TPU v7x, 32 devices: a whole 2x2x4 slice. The times are simulated.
32 devices in a mesh: dp: 2 (over x), expert: 4 (over z), mp: 4 (over y, core).
Axes of the slice: x: 2, y: 2, z: 4, core: 2. Of those that a mesh axis runs over, the one named last changes fastest.
Arguments:
- tokens: bfloat16 [128, 4096], P(('dp', 'expert', 'mp')), may hold values from -6 to 6
- probes: bfloat16 [2, 128, 4096], P(None, ('dp', 'expert', 'mp')), may hold values from -6 to 6
- cotangent: bfloat16 [128, 4096], P(('dp', 'expert', 'mp')), may hold values from -0.119628906 to 0.119628906
- expert_ids: int32 [128, 2], P(('dp', 'expert', 'mp')), may hold values from 0 to 3, all different within a row; in each aligned block of 4 rows (0 to 3, 4 to 7, ...) at most 4 rows name the same one
- combine: float32 [128, 2], P(('dp', 'expert', 'mp')), may hold values from 0.2 to 1
- w_gate: bfloat16 [4, 4096, 14336], P('expert', None, ('dp', 'mp')), may hold values from -0.09375 to 0.09375
- w_up: bfloat16 [4, 4096, 14336], P('expert', None, ('dp', 'mp')), may hold values from -0.09375 to 0.09375
- w_down: bfloat16 [4, 14336, 4096], P('expert', ('dp', 'mp')), may hold values from -0.046875 to 0.046875
Outputs:
- quad: float32 [2, 128], P(None, ('dp', 'expert', 'mp'))
Inputs may be any that keep to these rules, and one draw needn't show every extreme that they name: `expert_ids`: each token names 2 different experts. In each aligned block of 4 tokens (the tokens of one device) no expert is named by more than 4 of them, and some block reaches 4.
All inputs are finite; a program needn't handle non-finite values.
Results may differ from a plain program's by a relative error of at most 0.003.
Values may be sent and summed in bfloat16 or wider, within the bound.
No kernel may reach another device: no remote copies, remote signals or barrier semaphores. Data moves between devices by JAX's collectives and lax.ppermute only.
A program may use at most 128 MiB of HBM per device.

v0:
```python
import jax
import jax.numpy as jnp
from jax import lax
from jax.sharding import PartitionSpec as P


def silu_slopes(preact):
    squash = jax.nn.sigmoid(preact)
    first_slope = squash * (1.0 + preact * (1.0 - squash))
    second_slope = squash * (1.0 - squash) * (2.0 + preact * (1.0 - 2.0 * squash))
    return (first_slope, second_slope)


def on_device(tokens, probes, cotangent, expert_ids, combine, w_gate, w_up, w_down):
    tok_dev, model_width = tokens.shape
    probe_count = probes.shape[0]
    top_count = expert_ids.shape[1]
    experts = lax.axis_size("expert") * w_gate.shape[0]
    capacity = 2 * max(1, tok_dev * top_count // experts)
    routed = tok_dev * top_count
    flat_ids = expert_ids.reshape(routed)
    positions = jnp.arange(routed, dtype=jnp.int32)
    same_expert = flat_ids[:, None] == flat_ids[None, :]
    before = positions[None, :] < positions[:, None]
    slot_index = jnp.sum((same_expert & before).astype(jnp.int32), axis=1)
    expert_hot = flat_ids[:, None] == jnp.arange(experts, dtype=jnp.int32)[None, :]
    slot_hot = slot_index[:, None] == jnp.arange(capacity, dtype=jnp.int32)[None, :]
    placing = (expert_hot[:, :, None] & slot_hot[:, None, :]).reshape(routed, experts * capacity)
    scaled = (
        combine.reshape(routed, 1) * jnp.repeat(cotangent.astype(jnp.float32), top_count, axis=0)
    ).astype(jnp.bfloat16)
    stacked = jnp.repeat(jnp.concatenate([tokens[None], probes], axis=0), top_count, axis=1)
    stacked = jnp.concatenate([stacked, scaled[None]], axis=0)
    outgoing = jnp.einsum(
        "nk,rnd->rkd", placing.astype(jnp.bfloat16), stacked, preferred_element_type=jnp.float32
    ).astype(jnp.bfloat16)
    outgoing = outgoing.reshape(probe_count + 2, experts, capacity, model_width)
    arrived = lax.all_to_all(outgoing, "expert", split_axis=1, concat_axis=1, tiled=True)
    arrived = arrived.reshape(probe_count + 2, experts * capacity, model_width)
    gate_local = w_gate[0]
    up_local = w_up[0]
    down_local = w_down[0]
    block_rows = lax.all_gather(arrived, ("dp", "mp"), axis=1, tiled=True)
    row_count = block_rows.shape[1]
    base_rows = block_rows[0]
    tangent = block_rows[1 : probe_count + 1].reshape(probe_count * row_count, model_width)
    readout_rows = block_rows[probe_count + 1]
    gate_pre = jnp.dot(base_rows, gate_local, preferred_element_type=jnp.float32)
    up_pre = jnp.dot(base_rows, up_local, preferred_element_type=jnp.float32)
    readout = lax.dot_general(
        readout_rows, down_local, (((1,), (1,)), ((), ())), preferred_element_type=jnp.float32
    )
    gate_tan = jnp.dot(tangent, gate_local, preferred_element_type=jnp.float32).reshape(
        probe_count, row_count, -1
    )
    up_tan = jnp.dot(tangent, up_local, preferred_element_type=jnp.float32).reshape(
        probe_count, row_count, -1
    )
    first_slope, second_slope = silu_slopes(gate_pre)
    curved = second_slope * gate_tan * gate_tan * up_pre + 2.0 * first_slope * gate_tan * up_tan
    partial_quad = jnp.sum(curved * readout, axis=2)
    spread = partial_quad.reshape(probe_count, -1, experts, capacity)
    swapped = lax.all_to_all(spread, "expert", split_axis=2, concat_axis=2, tiled=True)
    returned_table = lax.psum_scatter(swapped, ("dp", "mp"), scatter_dimension=1, tiled=True)
    returned_table = returned_table.reshape(probe_count, experts * capacity)
    per_choice = jnp.dot(
        returned_table, placing.astype(jnp.float32).T, precision=lax.Precision.HIGHEST
    )
    return jnp.sum(per_choice.reshape(probe_count, tok_dev, top_count), axis=2)


def solution(mesh):
    in_specs = (
        P(("dp", "expert", "mp"), None),
        P(None, ("dp", "expert", "mp"), None),
        P(("dp", "expert", "mp"), None),
        P(("dp", "expert", "mp"), None),
        P(("dp", "expert", "mp"), None),
        P("expert", None, ("dp", "mp")),
        P("expert", None, ("dp", "mp")),
        P("expert", ("dp", "mp"), None),
    )
    out_specs = P(None, ("dp", "expert", "mp"))
    return jax.shard_map(
        on_device, mesh=mesh, in_specs=in_specs, out_specs=out_specs, check_vma=False
    )
```

profile of v0, /device:TPU:0, one launch (start us, length us, event | category | flops | bytes accessed | tf_op | source)
XLA Modules:
  0.0 151.4 jit_solution(9629628665399387584)
XLA Ops:
  6.5 0.0 all-gather.2.cloned.1.call-start
  6.5 0.8 copy.29
  7.3 0.1 eq.49
  7.4 0.2 convert_reduce_fusion
  7.6 0.1 iota_compare_fusion
  7.6 0.1 broadcast_and_fusion
  7.7 0.1 copy.30
  7.9 0.8 copy.28
  8.6 0.1 mul.76
  8.7 0.9 pad_maximum_fusion
  9.6 0.1 broadcast_in_dim.7
  9.8 0.1 reshape.132
  9.8 0.8 broadcast_in_dim.8
  10.6 0.1 reshape.133
  10.7 0.1 multiply_convert_fusion
  10.8 0.3 fusion.10
  11.1 0.2 reshape.134
  11.3 0.2 copy.32
  11.5 20.6 %all_to_all.10 = bf16[4,4,4,4096]{3,2,0,1:T(4,128)(2,1)S(1)} all-to-all(bf16[4,4,4,4096]{3,2,0,1:T(4,128)(2,1)S(1)} %copy.32), channel_id=1, replica_groups=mesh['dp'=2,'expert'=4,'mp'=4] {'expert'}, dimensions={1} | all-to-all | bytes 1048576 | tf_op jit(solution)/shard_map/all_to_all | solution.py:38
  32.2 0.2 copy.33
  32.4 0.9 reshape.135
  33.3 0.0 all-gather.2.cloned.1.call-update
  33.3 35.8 %all-gather.2.cloned.1.call-done = bf16[4,128,4096]{2,1,0:T(8,128)(2,1)} async-done(((bf16[4,16,4096]{2,1,0:T(8,128)(2,1)}), bf16[4,128,4096]{2,1,0:T(8,128)(2,1)}) %all-gather.2.cloned.1.call-update) | async-done | bytes 4194320 | tf_op jit(solution)/shard_map/all_gather | solution.py:43
  69.2 0.0 copy-start
  69.2 0.0 slice-start
  69.2 0.0 slice-start.1
  69.2 0.0 slice-start.2
  69.2 8.7 %fusion.6 = f32[2,128,1792]{2,1,0:T(8,128)S(1)} fusion(bf16[4,128,4096]{2,1,0:T(8,128)(2,1)} %all-gather.2.cloned.1.call-done, bf16[1,4096,1792]{2,1,0:T(8,128)(2,1)} %param.13), kind=kOutput, calls=%fused_computation.6 | convolution fusion | flops 3758096384 | bytes 20709376 | tf_op jit(solution)/shard_map/dot_general | solution.py:53
  77.9 0.0 copy-done
  77.9 0.0 slice-start.3
  77.9 9.5 %fusion.24 = (f32[128,1792]{1,0:T(8,128)S(1)}, f32[128,1792]{1,0:T(8,128)}) fusion(bf16[1,4096,1792]{2,1,0:T(8,128)(2,1)} %param.13, bf16[4,128,4096]{2,1,0:T(8,128)(2,1)S(1)} %copy-done), kind=kOutput, calls=%fused_computation.23 | convolution fusion | flops 1882259456 | bytes 17563648 | tf_op jit(solution)/shard_map/dot_general | solution.py:48
  87.4 0.0 slice-done
  87.4 0.0 slice-done.1
  87.4 0.0 slice-done.2
  87.4 0.0 slice-done.3
  87.5 2.2 %fusion.4 = f32[128,1792]{1,0:T(8,128)S(1)} fusion(bf16[1,4096,1792]{2,1,0:T(8,128)(2,1)S(1)} %bitcast.48, bf16[4,128,4096]{2,1,0:T(8,128)(2,1)S(1)} %copy-done), kind=kOutput, calls=%fused_computation.4 | convolution fusion | flops 1879048192 | bytes 16646144 | tf_op jit(solution)/shard_map/dot_general | solution.py:49
  89.6 10.1 %fusion = f32[128,1792]{1,0:T(8,128)S(1)} fusion(bf16[1,1792,4096]{2,1,0:T(8,128)(2,1)} %param.15, bf16[4,128,4096]{2,1,0:T(8,128)(2,1)S(1)} %copy-done), kind=kOutput, calls=%fused_computation | convolution fusion | flops 1879048192 | bytes 16646144 | tf_op jit(solution)/shard_map/dot_general | solution.py:50
  99.8 0.0 copy-start.1
  99.8 9.7 %fusion.21 = f32[2,128]{1,0:T(2,128)S(1)} fusion(bf16[4,128,4096]{2,1,0:T(8,128)(2,1)S(1)} %copy-done, bf16[1,4096,1792]{2,1,0:T(8,128)(2,1)} %param.14, f32[2,128,1792]{2,1,0:T(8,128)S(1)} %fusion.6, f32[128,1792]{1,0:T(8,128)S(1)} %fusion, f32[128,1792]{1,0:T(8,128)} %get-tuple-element.6, f32[128,1792]{1,0:T(8,128)S(1)} %fusion.4, ...), kind=kOutput, calls=%fused_computation.17 | convolution fusion | flops 3761766144 | bytes 24380416 | tf_op jit(solution)/shard_map/dot_general | solution.py:56
  109.5 0.1 reshape.136
  109.6 0.7 copy.34
  110.3 4.6 %all-to-all-start.1 = ((f32[2,8,4,4]{1,3,0,2:T(4,128)}), f32[2,8,4,4]{1,3,0,2:T(4,128)S(1)}, u32[]{:S(2)}, u32[]{:S(2)}) async-start(f32[2,8,4,4]{1,3,0,2:T(4,128)} %copy.34), calls=%async_computation.1 | async-start | bytes 32768 | tf_op jit(solution)/shard_map/all_to_all | solution.py:63
  114.9 0.1 and.35
  115.0 0.0 copy-done.1
  115.0 0.6 dynamic-slice
  115.6 4.9 %all-to-all-done.1 = f32[2,8,4,4]{1,3,0,2:T(4,128)S(1)} async-done(((f32[2,8,4,4]{1,3,0,2:T(4,128)}), f32[2,8,4,4]{1,3,0,2:T(4,128)S(1)}, u32[]{:S(2)}, u32[]{:S(2)}) %all-to-all-start.1) | async-done | bytes 1056 | tf_op jit(solution)/shard_map/all_to_all | solution.py:63
  120.6 0.1 copy.35
  120.7 22.3 %all-reduce = f32[2,8,4,4]{3,2,1,0:T(4,128)S(1)} all-reduce(f32[2,8,4,4]{3,2,1,0:T(4,128)S(1)} %copy.35), channel_id=2, replica_groups=mesh['dp'=2,'expert'=4,'mp'=4] {'dp','mp'}, use_global_device_ids=true, to_apply=%region_2.0.clone | all-reduce | flops 256 | bytes 2048
  143.0 0.6 constant_dynamic-slice_fusion
  143.7 0.1 reshape.141
  143.8 0.8 convolution_reduce_fusion
  (1 shorter events, 0.0 us)
Async XLA Ops:
  6.5 62.6 %all-gather.2.cloned.1.call-start = ((), (), s32[]{:S(2)}) async-start(), calls=%async_computation.2 | async-start | bytes 4718592 | tf_op jit(solution)/shard_map/all_gather | solution.py:43
  69.2 8.8 %copy-start = (bf16[4,128,4096]{2,1,0:T(8,128)(2,1)S(1)}, bf16[4,128,4096]{2,1,0:T(8,128)(2,1)}, u32[]{:S(2)}) copy-start(bf16[4,128,4096]{2,1,0:T(8,128)(2,1)} %all-gather.2.cloned.1.call-done) | copy-start | bytes 12582916
  69.2 18.3 %slice-start = ((s8[14680064]{0:T(1024)(128)(4,1)}), s8[4194304]{0:T(1024)(128)(4,1)S(1)}, s32[]{:S(2)}) async-start(s8[14680064]{0:T(1024)(128)(4,1)} %bitcast.47), calls=%async_computation.3 | async-start | bytes 8388608
  69.2 18.3 %slice-start.1 = ((s8[14680064]{0:T(1024)(128)(4,1)}), s8[4194304]{0:T(1024)(128)(4,1)S(1)}, s32[]{:S(2)}) async-start(s8[14680064]{0:T(1024)(128)(4,1)} %bitcast.47), calls=%async_computation.4 | async-start | bytes 8388608
  69.2 18.3 %slice-start.2 = ((s8[14680064]{0:T(1024)(128)(4,1)}), s8[4194304]{0:T(1024)(128)(4,1)S(1)}, s32[]{:S(2)}) async-start(s8[14680064]{0:T(1024)(128)(4,1)} %bitcast.47), calls=%async_computation.5 | async-start | bytes 8388608
  77.9 9.5 %slice-start.3 = ((s8[14680064]{0:T(1024)(128)(4,1)}), s8[2097152]{0:T(1024)(128)(4,1)S(1)}, s32[]{:S(2)}) async-start(s8[14680064]{0:T(1024)(128)(4,1)} %bitcast.47), calls=%async_computation.6 | async-start | bytes 4194304
  99.8 15.2 %copy-start.1 = (u32[32]{0:T(128)S(1)}, u32[32]{0:T(128)}, u32[]{:S(2)}) copy-start(u32[32]{0:T(128)} %constant.18) | copy-start | bytes 388
  110.3 10.2 %all-to-all-start.1 = ((f32[2,8,4,4]{1,3,0,2:T(4,128)}), f32[2,8,4,4]{1,3,0,2:T(4,128)S(1)}, u32[]{:S(2)}, u32[]{:S(2)}) async-start(f32[2,8,4,4]{1,3,0,2:T(4,128)} %copy.34), calls=%async_computation.1 | async-start | bytes 32768 | tf_op jit(solution)/shard_map/all_to_all | solution.py:63
Sparse Core Ops, SparseCore 0:
  33.4 35.6 all-gather.1
where the time goes:
time: 152 us; the launch traced here: 151 us
  blocking collectives  43 us (28%)
  matrix products  41.3 us (27%)
  waiting for transfers between devices  40.8 us (27%)
  between operations  13.5 us (9%)
  local copies, waits for them, and re-layouts  6.85 us (5%)
  starting transfers between devices  4.6 us (3%)
    all_gather x1, waiting for transfers between devices, on_device(): block_rows = lax.all_gather(arrived, ('dp', 'mp'), axis=1, tiled=True)  35.8 us
    unnamed x1, blocking collectives  22.3 us
    all_to_all x1, blocking collectives, on_device(): lax.all_to_all(outgoing, 'expert', split_axis=1, concat_axis=1, tiled=True)  20.6 us
    dot_general x1, matrix products, on_device(): lax.dot_general(readout_rows, down_local, (((1,), (1,)), ((), ())), prefe...  10.1 us
    dot_general x1, matrix products, on_device(): jnp.dot(tangent, up_local, preferred_element_type=jnp.float32)  9.69 us
    dot_general x1, matrix products, on_device(): jnp.dot(base_rows, gate_local, preferred_element_type=jnp.float32)  9.49 us
    dot_general x1, matrix products, on_device(): jnp.dot(tangent, gate_local, preferred_element_type=jnp.float32)  8.75 us
    all_to_all x1, waiting for transfers between devices, on_device(): lax.all_to_all(spread, 'expert', split_axis=2, concat_axis=2, tiled=True)  4.94 us
  transfers between devices with their start and end apart: 2, of which 2 were waited for; matrix products, arithmetic and copies ran while one was open for 0% of the time, Pallas kernels for 0%

commit v1 on v0

--- a/solution.py
+++ b/solution.py
@@ -2,6 +2,16 @@
 import jax.numpy as jnp
 from jax import lax
 from jax.sharding import PartitionSpec as P
+
+rest_the_blocks = lambda z: jnp.concatenate(
+    lax.all_to_all(
+        jnp.stack(jnp.split(z, lax.psum(1, axis_name="expert"), axis=1)),
+        axis_name="expert",
+        split_axis=0,
+        concat_axis=0,
+    ),
+    axis=1,
+)
 
 
 def silu_slopes(preact):
@@ -35,7 +45,7 @@
         "nk,rnd->rkd", placing.astype(jnp.bfloat16), stacked, preferred_element_type=jnp.float32
     ).astype(jnp.bfloat16)
     outgoing = outgoing.reshape(probe_count + 2, experts, capacity, model_width)
-    arrived = lax.all_to_all(outgoing, "expert", split_axis=1, concat_axis=1, tiled=True)
+    arrived = rest_the_blocks(outgoing)
     arrived = arrived.reshape(probe_count + 2, experts * capacity, model_width)
     gate_local = w_gate[0]
     up_local = w_up[0]

time: 152 us -> 152 us (level)
  no operation moved by 1% of the time
where the time goes in v1:
time: 152 us
  blocking collectives  43 us (28%)
  matrix products  41.4 us (27%)
  waiting for transfers between devices  40.8 us (27%)
  between operations  13.6 us (9%)
  local copies, waits for them, and re-layouts  6.85 us (5%)
  starting transfers between devices  4.6 us (3%)
  other arithmetic  1.8 us (1%)
    all_gather x1, waiting for transfers between devices, on_device(): block_rows = lax.all_gather(arrived, ('dp', 'mp'), axis=1, tiled=True)  35.8 us
    unnamed x1, blocking collectives  22.3 us
    all_to_all x1, blocking collectives, lax.all_to_all(jnp.stack(jnp.split(z, lax.psum(1, axis_name='expert'), ax...  20.6 us
    dot_general x1, matrix products, on_device(): lax.dot_general(readout_rows, down_local, (((1,), (1,)), ((), ())), prefe...  10.1 us
    dot_general x1, matrix products, on_device(): jnp.dot(tangent, up_local, preferred_element_type=jnp.float32)  9.77 us
    dot_general x1, matrix products, on_device(): jnp.dot(base_rows, gate_local, preferred_element_type=jnp.float32)  9.51 us
    dot_general x1, matrix products, on_device(): jnp.dot(tangent, gate_local, preferred_element_type=jnp.float32)  8.75 us
    all_to_all x1, waiting for transfers between devices, on_device(): lax.all_to_all(spread, 'expert', split_axis=2, concat_axis=2, tiled=True)  4.94 us
  transfers between devices with their start and end apart: 2, of which 2 were waited for; matrix products, arithmetic and copies ran while one was open for 0% of the time, Pallas kernels for 0%

profile of v1, /device:TPU:0, one launch (start us, length us, event | category | flops | bytes accessed | tf_op | source)
XLA Modules:
  0.0 152.0 jit_solution(13193229490154965615)
XLA Ops:
  6.5 0.0 all-gather.2.cloned.1.call-start
  6.5 0.8 copy.39
  7.3 0.1 eq.49
  7.4 0.2 convert_reduce_fusion
  7.6 0.1 iota_compare_fusion
  7.6 0.1 broadcast_and_fusion
  7.7 0.1 copy.40
  7.9 0.8 copy.38
  8.6 0.1 mul.76
  8.7 0.9 pad_maximum_fusion.1
  9.6 0.1 broadcast_in_dim.7
  9.8 0.1 reshape.132
  9.8 0.8 broadcast_in_dim.8
  10.6 0.1 reshape.133
  10.7 0.1 multiply_convert_fusion
  10.8 0.3 fusion.10
  11.1 0.2 reshape.134
  11.3 0.2 slice_bitcast_fusion.8
  11.5 0.5 pad_maximum_fusion
  12.0 20.6 %all_to_all.10 = bf16[4,4,1,4,4096]{4,3,1,2,0:T(4,128)(2,1)S(1)} all-to-all(bf16[4,4,1,4,4096]{4,3,1,2,0:T(4,128)(2,1)S(1)} %pad_maximum_fusion), channel_id=1, replica_groups=mesh['dp'=2,'expert'=4,'mp'=4] {'expert'}, dimensions={0} | all-to-all | bytes 1048576 | tf_op jit(solution)/shard_map/all_to_all | solution.py:7
  32.6 0.2 copy.45
  32.8 0.9 reshape_reshape.3
  33.8 0.0 all-gather.2.cloned.1.call-update
  33.8 35.8 %all-gather.2.cloned.1.call-done = bf16[4,128,4096]{2,1,0:T(8,128)(2,1)} async-done(((bf16[4,16,4096]{2,1,0:T(8,128)(2,1)}), bf16[4,128,4096]{2,1,0:T(8,128)(2,1)}) %all-gather.2.cloned.1.call-update) | async-done | bytes 4194320 | tf_op jit(solution)/shard_map/all_gather | solution.py:53
  69.6 0.0 copy-start
  69.6 0.0 slice-start
  69.6 0.0 slice-start.1
  69.6 0.0 slice-start.2
  69.6 8.8 %fusion.6 = f32[2,128,1792]{2,1,0:T(8,128)S(1)} fusion(bf16[4,128,4096]{2,1,0:T(8,128)(2,1)} %all-gather.2.cloned.1.call-done, bf16[1,4096,1792]{2,1,0:T(8,128)(2,1)} %param.13), kind=kOutput, calls=%fused_computation.6 | convolution fusion | flops 3758096384 | bytes 20709376 | tf_op jit(solution)/shard_map/dot_general | solution.py:63
  78.4 0.0 copy-done
  78.4 0.0 slice-start.3
  78.4 9.5 %fusion.24 = (f32[128,1792]{1,0:T(8,128)S(1)}, f32[128,1792]{1,0:T(8,128)}) fusion(bf16[1,4096,1792]{2,1,0:T(8,128)(2,1)} %param.13, bf16[4,128,4096]{2,1,0:T(8,128)(2,1)S(1)} %copy-done), kind=kOutput, calls=%fused_computation.23 | convolution fusion | flops 1882259456 | bytes 17563648 | tf_op jit(solution)/shard_map/dot_general | solution.py:58
  87.9 0.0 slice-done
  87.9 0.0 slice-done.1
  87.9 0.0 slice-done.2
  87.9 0.0 slice-done.3
  88.0 2.2 %fusion.4 = f32[128,1792]{1,0:T(8,128)S(1)} fusion(bf16[1,4096,1792]{2,1,0:T(8,128)(2,1)S(1)} %bitcast.65, bf16[4,128,4096]{2,1,0:T(8,128)(2,1)S(1)} %copy-done), kind=kOutput, calls=%fused_computation.4 | convolution fusion | flops 1879048192 | bytes 16646144 | tf_op jit(solution)/shard_map/dot_general | solution.py:59
  90.2 10.1 %fusion = f32[128,1792]{1,0:T(8,128)S(1)} fusion(bf16[1,1792,4096]{2,1,0:T(8,128)(2,1)} %param.15, bf16[4,128,4096]{2,1,0:T(8,128)(2,1)S(1)} %copy-done), kind=kOutput, calls=%fused_computation | convolution fusion | flops 1879048192 | bytes 16646144 | tf_op jit(solution)/shard_map/dot_general | solution.py:60
  100.3 0.0 copy-start.1
  100.4 9.8 %fusion.21 = f32[2,128]{1,0:T(2,128)S(1)} fusion(bf16[4,128,4096]{2,1,0:T(8,128)(2,1)S(1)} %copy-done, bf16[1,4096,1792]{2,1,0:T(8,128)(2,1)} %param.14, f32[2,128,1792]{2,1,0:T(8,128)S(1)} %fusion.6, f32[128,1792]{1,0:T(8,128)S(1)} %fusion, f32[128,1792]{1,0:T(8,128)} %get-tuple-element.6, f32[128,1792]{1,0:T(8,128)S(1)} %fusion.4, ...), kind=kOutput, calls=%fused_computation.17 | convolution fusion | flops 3761766144 | bytes 24380416 | tf_op jit(solution)/shard_map/dot_general | solution.py:66
  110.1 0.1 reshape.136
  110.2 0.7 copy.46
  111.0 4.6 %all-to-all-start.1 = ((f32[2,8,4,4]{1,3,0,2:T(4,128)}), f32[2,8,4,4]{1,3,0,2:T(4,128)S(1)}, u32[]{:S(2)}, u32[]{:S(2)}) async-start(f32[2,8,4,4]{1,3,0,2:T(4,128)} %copy.46), calls=%async_computation.1 | async-start | bytes 32768 | tf_op jit(solution)/shard_map/all_to_all | solution.py:73
  115.6 0.1 and.35
  115.7 0.0 copy-done.1
  115.7 0.6 dynamic-slice
  116.3 4.9 %all-to-all-done.1 = f32[2,8,4,4]{1,3,0,2:T(4,128)S(1)} async-done(((f32[2,8,4,4]{1,3,0,2:T(4,128)}), f32[2,8,4,4]{1,3,0,2:T(4,128)S(1)}, u32[]{:S(2)}, u32[]{:S(2)}) %all-to-all-start.1) | async-done | bytes 1056 | tf_op jit(solution)/shard_map/all_to_all | solution.py:73
  121.2 0.1 copy.47
  121.3 22.3 %all-reduce = f32[2,8,4,4]{3,2,1,0:T(4,128)S(1)} all-reduce(f32[2,8,4,4]{3,2,1,0:T(4,128)S(1)} %copy.47), channel_id=2, replica_groups=mesh['dp'=2,'expert'=4,'mp'=4] {'dp','mp'}, use_global_device_ids=true, to_apply=%region_2.0.clone | all-reduce | flops 256 | bytes 2048
  143.7 0.6 constant_dynamic-slice_fusion
  144.3 0.1 reshape.141
  144.4 0.8 convolution_reduce_fusion
  (1 shorter events, 0.0 us)
Async XLA Ops:
  6.5 63.1 %all-gather.2.cloned.1.call-start = ((), (), s32[]{:S(2)}) async-start(), calls=%async_computation.2 | async-start | bytes 4718592 | tf_op jit(solution)/shard_map/all_gather | solution.py:53
  69.6 8.8 %copy-start = (bf16[4,128,4096]{2,1,0:T(8,128)(2,1)S(1)}, bf16[4,128,4096]{2,1,0:T(8,128)(2,1)}, u32[]{:S(2)}) copy-start(bf16[4,128,4096]{2,1,0:T(8,128)(2,1)} %all-gather.2.cloned.1.call-done) | copy-start | bytes 12582916
  69.6 18.3 %slice-start = ((s8[14680064]{0:T(1024)(128)(4,1)}), s8[4194304]{0:T(1024)(128)(4,1)S(1)}, s32[]{:S(2)}) async-start(s8[14680064]{0:T(1024)(128)(4,1)} %bitcast.64), calls=%async_computation.3 | async-start | bytes 8388608
  69.6 18.3 %slice-start.1 = ((s8[14680064]{0:T(1024)(128)(4,1)}), s8[4194304]{0:T(1024)(128)(4,1)S(1)}, s32[]{:S(2)}) async-start(s8[14680064]{0:T(1024)(128)(4,1)} %bitcast.64), calls=%async_computation.4 | async-start | bytes 8388608
  69.6 18.3 %slice-start.2 = ((s8[14680064]{0:T(1024)(128)(4,1)}), s8[4194304]{0:T(1024)(128)(4,1)S(1)}, s32[]{:S(2)}) async-start(s8[14680064]{0:T(1024)(128)(4,1)} %bitcast.64), calls=%async_computation.5 | async-start | bytes 8388608
  78.4 9.5 %slice-start.3 = ((s8[14680064]{0:T(1024)(128)(4,1)}), s8[2097152]{0:T(1024)(128)(4,1)S(1)}, s32[]{:S(2)}) async-start(s8[14680064]{0:T(1024)(128)(4,1)} %bitcast.64), calls=%async_computation.6 | async-start | bytes 4194304
  100.3 15.3 %copy-start.1 = (u32[32]{0:T(128)S(1)}, u32[32]{0:T(128)}, u32[]{:S(2)}) copy-start(u32[32]{0:T(128)} %constant.18) | copy-start | bytes 388
  111.0 10.2 %all-to-all-start.1 = ((f32[2,8,4,4]{1,3,0,2:T(4,128)}), f32[2,8,4,4]{1,3,0,2:T(4,128)S(1)}, u32[]{:S(2)}, u32[]{:S(2)}) async-start(f32[2,8,4,4]{1,3,0,2:T(4,128)} %copy.46), calls=%async_computation.1 | async-start | bytes 32768 | tf_op jit(solution)/shard_map/all_to_all | solution.py:73
Sparse Core Ops, SparseCore 0:
  33.9 35.6 all-gather.1
